TPU v7x, 512 devices: a whole 4x8x8 slice. The times are simulated.
512 devices in a mesh: ens: 4 (over z_lo), replica: 32 (over y_lo, x, core), model: 4 (over z_hi, y_hi).
Axes of the slice: x: 4, y: 8 (y_hi: 2, y_lo: 4; y = y_hi * 4 + y_lo), z: 8 (z_hi: 2, z_lo: 4; z = z_hi * 4 + z_lo), core: 2. Of those that a mesh axis runs over, the one named last changes fastest.
Arguments:
- slope_up: float32 [128, 768, 3072], P(('ens', 'replica'), None, 'model'), parts along dimension 0, may hold values from -1.25 to 1.25
- slope_down: float32 [128, 3072, 768], P(('ens', 'replica'), 'model'), parts along dimension 0, may hold values from -1.25 to 1.25
- slope_norm: float32 [128, 768], P(('ens', 'replica')), parts along dimension 0, may hold values from -12 to 12
- slope_bias: float32 [128, 768], P(('ens', 'replica')), parts along dimension 0, may hold values from -12 to 12
- param_up: float32 [3072, 3072], P(('ens', 'replica'), 'model'), parts along dimension 0, may hold values from -0.4375 to 0.4375
- param_down: float32 [12288, 768], P(('ens', 'model'), 'replica'), parts along dimension 0, may hold values from -0.21875 to 0.21875
- param_norm: float32 [3072], P(('ens', 'replica')), parts along dimension 0, may hold values from 0.25 to 1.75
- param_bias: float32 [3072], P(('ens', 'replica')), parts along dimension 0, may hold values from -3 to 3
Outputs:
- half_up: bfloat16 [3072, 3072], P('ens', 'model'), parts along dimension 0
- half_down: bfloat16 [12288, 768], P(('ens', 'model')), parts along dimension 0
- half_norm: bfloat16 [3072], P('ens'), parts along dimension 0
- half_bias: bfloat16 [3072], P('ens'), parts along dimension 0
- next_up: float32 [3072, 3072], P(('ens', 'replica'), 'model'), parts along dimension 0
- next_down: float32 [12288, 768], P(('ens', 'model'), 'replica'), parts along dimension 0
- next_norm: float32 [3072], P(('ens', 'replica')), parts along dimension 0
- next_bias: float32 [3072], P(('ens', 'replica')), parts along dimension 0
There are 4 independent parts, one for each index of `ens`. A program takes and returns all parts, laid end to end along the dimension named above; each array names one. Nothing has to cross between parts.
All inputs are finite; a program needn't handle non-finite values.
Results may differ from a plain program's by a relative error of at most 0.0004.
Values may be sent and summed in bfloat16 or wider, within the bound.
No kernel may reach another device: no remote copies, remote signals or barrier semaphores. Data moves between devices by JAX's collectives and lax.ppermute only.
A program may use at most 64 MiB of HBM per device.

v0:
```python
import jax
import jax.numpy as jnp
from jax import lax
from jax.sharding import Mesh
from jax.sharding import PartitionSpec as P

REPLICA = ("replica_0", "replica_1", "replica_2")
ENS_REPLICA = ("ens", "replica_0", "replica_1", "replica_2")
learn_rate = 0.4


def split_up(shard, dim, count):
    lengths = shard.shape
    tiles = shard.reshape(*lengths[:dim], count, lengths[dim] // count, *lengths[dim + 1 :])
    return jnp.moveaxis(tiles, dim, 0)


def sum_at_owner(shard, axis, dim):
    count = lax.axis_size(axis)
    tiles = lax.all_to_all(split_up(shard, dim, count), axis, 0, 0, tiled=True)
    return jnp.sum(tiles, axis=0)


def sum_by_axis(shard, axes, dim):
    far, near = axes
    tiles = split_up(shard, dim, lax.axis_size(far))
    nearer = sum_at_owner(tiles, near, dim + 1)
    arrived = lax.all_to_all(nearer, far, split_axis=0, concat_axis=0, tiled=True)
    return arrived.sum(axis=0)


def from_everyone(shard, axis):
    count = lax.axis_size(axis)
    return lax.all_to_all(
        jnp.broadcast_to(shard[None], (count, *shard.shape)), axis, 0, 0, tiled=True
    )


def taken_together(shard, axis):
    return from_everyone(shard, axis).sum(axis=0)


def together(arrays, axis):
    ends = [0]
    for a in arrays:
        ends.append(ends[-1] + a.size)
    total = taken_together(jnp.concatenate([a.ravel() for a in arrays]), axis)
    return tuple((total[b:e].reshape(a.shape) for a, b, e in zip(arrays, ends, ends[1:])))


def gather_turned(arrays, axis, dims):
    turned = [jnp.moveaxis(a, dim, 0) for a, dim in zip(arrays, dims)]
    both = jnp.concatenate([t.reshape(len(t), -1) for t in turned], axis=1)
    whole, at, outs = (lax.all_gather(both, axis, axis=0, tiled=True), 0, [])
    for t, dim in zip(turned, dims):
        section = whole[:, at : at + t[0].size].reshape(-1, *t.shape[1:])
        outs.append(jnp.moveaxis(section, 0, dim))
        at += t[0].size
    return tuple(outs)


def on_device(
    slope_up, slope_down, slope_norm, slope_bias, param_up, param_down, param_norm, param_bias
):
    mean_up, mean_down, mean_norm, mean_bias = (
        sum_by_axis(slope_up[0], (("replica_0", "replica_1"), "replica_2"), 0),
        sum_by_axis(slope_down[0], (("replica_0", "replica_1"), "replica_2"), 1),
        sum_by_axis(slope_norm[0], (("replica_0", "replica_1"), "replica_2"), 0),
        sum_by_axis(slope_bias[0], (("replica_0", "replica_1"), "replica_2"), 0),
    )
    mean_rate = lax.axis_size(REPLICA) ** (-0.5)
    mean_up = mean_up * mean_rate
    mean_down = mean_down * mean_rate
    mean_norm = mean_norm * mean_rate
    mean_bias = mean_bias * mean_rate
    own_up, own_down, slope_up_norm, slope_down_norm = together(
        (
            jnp.sum(param_up * param_up, axis=1, keepdims=True),
            jnp.sum(param_down * param_down, axis=0, keepdims=True),
            jnp.sum(mean_up * mean_up, axis=1, keepdims=True),
            jnp.sum(mean_down * mean_down, axis=0, keepdims=True),
        ),
        "model",
    )
    mean_up = mean_up * (jnp.sqrt(own_up) * lax.rsqrt(slope_up_norm + 1e-06))
    mean_down = mean_down * (jnp.sqrt(own_down) * lax.rsqrt(slope_down_norm + 1e-06))
    next_up = param_up - learn_rate * mean_up
    next_down = param_down - learn_rate * mean_down
    next_norm = param_norm - learn_rate * mean_norm
    next_bias = param_bias - learn_rate * mean_bias
    half_up, half_down, half_norm, half_bias = gather_turned(
        (
            next_up.astype(jnp.bfloat16),
            next_down.astype(jnp.bfloat16),
            next_norm.astype(jnp.bfloat16),
            next_bias.astype(jnp.bfloat16),
        ),
        REPLICA,
        (0, 1, 0, 0),
    )
    return (half_up, half_down, half_norm, half_bias, next_up, next_down, next_norm, next_bias)


def solution(mesh):
    split = Mesh(
        mesh.devices.reshape(mesh.shape["ens"], 4, 4, 2, mesh.shape["model"]),
        ("ens", "replica_0", "replica_1", "replica_2", "model"),
    )
    placed = (
        P(ENS_REPLICA, None, "model"),
        P(ENS_REPLICA, "model", None),
        P(ENS_REPLICA, None),
        P(ENS_REPLICA, None),
        P(ENS_REPLICA, "model"),
        P(("ens", "model"), REPLICA),
        P(ENS_REPLICA),
        P(ENS_REPLICA),
    )
    return jax.shard_map(
        on_device,
        mesh=split,
        in_specs=placed,
        out_specs=(
            P("ens", "model"),
            P(("ens", "model"), None),
            P("ens"),
            P("ens"),
            P(ENS_REPLICA, "model"),
            P(("ens", "model"), REPLICA),
            P(ENS_REPLICA),
            P(ENS_REPLICA),
        ),
        check_vma=False,
    )
```

profile of v0, /device:TPU:1, one launch (start us, length us, event | category | flops | bytes accessed | tf_op | source)
XLA Modules:
  0.0 228.4 jit_solution(1284755570534542590)
XLA Ops:
  7.2 0.7 reduce.3
  7.9 0.1 reshape_reshape_squeeze.10
  8.0 0.7 reshape.64
  8.6 10.0 %all-to-all-start.5 = ((f32[2,1,384]{2,1,0:T(1,128)}), f32[2,1,384]{2,1,0:T(1,128)S(1)}, u32[]{:S(2)}, u32[]{:S(2)}) async-start(f32[2,1,384]{2,1,0:T(1,128)} %reshape.64), calls=%async_computation.5 | async-start | bytes 6144 | tf_op jit(solution)/shard_map/all_to_all | solution.py:20
  18.7 0.7 reduce.4
  19.4 0.1 reshape_reshape_squeeze.11
  19.5 0.7 reshape.66
  20.2 3.2 %all-to-all-start.7 = ((f32[2,1,384]{2,1,0:T(1,128)}), f32[2,1,384]{2,1,0:T(1,128)S(1)}, u32[]{:S(2)}, u32[]{:S(2)}) async-start(f32[2,1,384]{2,1,0:T(1,128)} %reshape.66), calls=%async_computation.7 | async-start | bytes 6144 | tf_op jit(solution)/shard_map/all_to_all | solution.py:20
  23.4 0.5 broadcast.24
  23.9 0.7 reduce.9
  24.6 0.1 reshape.65
  24.7 1.8 copy.47
  26.5 3.0 %copy.48 = f32[1,768,768]{1,2,0:T(8,128)} copy(f32[1,768,768]{2,1,0:T(8,128)} %param.9) | data formatting | bytes 4718592 | tf_op args[1]
  29.6 3.3 %copy.49 = f32[2,16,768,24]{2,3,1,0:T(8,128)} copy(f32[2,16,768,24]{2,3,0,1:T(8,128)} %bitcast.23) | data formatting | bytes 4718592 | tf_op jit(solution)/shard_map/transpose | solution.py:15
  32.8 0.6 reduce_sum.126
  33.4 6.3 %all_to_all.54 = f32[2,16,24,768]{3,2,1,0:T(8,128)} all-to-all(f32[2,16,24,768]{3,2,1,0:T(8,128)S(1)} %copy.47), channel_id=1, replica_groups=mesh['ens'=4,'replica_0'=4,'replica_1'=4,'replica_2'=2,'model'=4] {'repl..., dimensions={0} | all-to-all | bytes 4718592 | tf_op jit(solution)/shard_map/all_to_all | solution.py:20
  39.7 5.6 %all_to_all.55 = f32[2,16,768,24]{2,3,1,0:T(8,128)S(1)} all-to-all(f32[2,16,768,24]{2,3,1,0:T(8,128)S(1)} %copy-done), channel_id=1, replica_groups=mesh['ens'=4,'replica_0'=4,'replica_1'=4,'replica_2'=2,'model'=4] {'repl..., dimensions={0} | all-to-all | bytes 4718592 | tf_op jit(solution)/shard_map/all_to_all | solution.py:20
  45.4 3.5 %all-to-all-start.6 = ((f32[16,1,24]{2,1,0:T(1,128)}), f32[16,1,24]{2,1,0:T(1,128)S(1)}, u32[]{:S(2)}, u32[]{:S(2)}) async-start(f32[16,1,24]{2,1,0:T(1,128)} %bitcast.9), calls=%async_computation.6 | async-start | bytes 16384 | tf_op jit(solution)/shard_map/all_to_all | solution.py:28
  48.8 0.7 reduce.10
  49.5 0.1 reshape.67
  49.6 0.6 reduce_sum.128
  50.2 5.3 %all-to-all-done.6 = f32[16,1,24]{2,1,0:T(1,128)S(1)} async-done(((f32[16,1,24]{2,1,0:T(1,128)}), f32[16,1,24]{2,1,0:T(1,128)S(1)}, u32[]{:S(2)}, u32[]{:S(2)}) %all-to-all-start.6) | async-done | bytes 1568 | tf_op jit(solution)/shard_map/all_to_all | solution.py:28
  55.5 3.5 %all-to-all-start.8 = ((f32[16,1,24]{2,1,0:T(1,128)}), f32[16,1,24]{2,1,0:T(1,128)S(1)}, u32[]{:S(2)}, u32[]{:S(2)}) async-start(f32[16,1,24]{2,1,0:T(1,128)} %bitcast.12), calls=%async_computation.8 | async-start | bytes 16384 | tf_op jit(solution)/shard_map/all_to_all | solution.py:28
  59.0 3.0 %reduce_sum.117 = f32[16,24,768]{2,1,0:T(8,128)} reduce(f32[2,16,24,768]{3,2,1,0:T(8,128)} %all_to_all.54, f32[]{:T(128)} %constant.5.clone.1), dimensions={0}, to_apply=%region_0.0 | reduce | flops 294912 | bytes 3538948 | tf_op jit(solution)/shard_map/reduce_sum | solution.py:21
  61.9 3.7 %all-to-all-done.8 = f32[16,1,24]{2,1,0:T(1,128)S(1)} async-done(((f32[16,1,24]{2,1,0:T(1,128)}), f32[16,1,24]{2,1,0:T(1,128)S(1)}, u32[]{:S(2)}, u32[]{:S(2)}) %all-to-all-start.8) | async-done | bytes 1568 | tf_op jit(solution)/shard_map/all_to_all | solution.py:28
  65.7 3.7 %all-to-all-start.1 = ((f32[16,24,768]{2,1,0:T(8,128)}), f32[16,24,768]{2,1,0:T(8,128)S(1)}, u32[]{:S(2)}, u32[]{:S(2)}) async-start(f32[16,24,768]{2,1,0:T(8,128)} %reduce_sum.117), calls=%async_computation.1 | async-start | bytes 2359296 | tf_op jit(solution)/shard_map/all_to_all | solution.py:28
  69.4 1.3 reduce_sum.122
  70.7 23.0 %all-to-all-done.1 = f32[16,24,768]{2,1,0:T(8,128)S(1)} async-done(((f32[16,24,768]{2,1,0:T(8,128)}), f32[16,24,768]{2,1,0:T(8,128)S(1)}, u32[]{:S(2)}, u32[]{:S(2)}) %all-to-all-start.1) | async-done | bytes 1179680 | tf_op jit(solution)/shard_map/all_to_all | solution.py:28
  93.7 8.4 %all-to-all-start.3 = ((f32[16,768,24]{1,2,0:T(8,128)}), f32[16,768,24]{1,2,0:T(8,128)S(1)}, u32[]{:S(2)}, u32[]{:S(2)}) async-start(f32[16,768,24]{1,2,0:T(8,128)} %reduce_sum.122), calls=%async_computation.3 | async-start | bytes 2359296 | tf_op jit(solution)/shard_map/all_to_all | solution.py:28
  102.1 0.1 multiply_reduce_fusion.3
  102.2 0.1 multiply_reduce_fusion.2
  102.4 0.5 convert_bitcast_fusion.2
  103.0 0.1 multiply_reduce_fusion.1
  103.1 23.3 %all-to-all-done.3 = f32[16,768,24]{1,2,0:T(8,128)S(1)} async-done(((f32[16,768,24]{1,2,0:T(8,128)}), f32[16,768,24]{1,2,0:T(8,128)S(1)}, u32[]{:S(2)}, u32[]{:S(2)}) %all-to-all-start.3) | async-done | bytes 1179680 | tf_op jit(solution)/shard_map/all_to_all | solution.py:28
  126.5 0.1 multiply_reduce_fusion
  126.7 0.6 broadcast_in_dim.2
  127.3 10.9 %all-to-all-start.4 = ((f32[4,1,96]{2,1,0:T(1,128)}), f32[4,1,96]{2,1,0:T(1,128)S(1)}, u32[]{:S(2)}, u32[]{:S(2)}) async-start(f32[4,1,96]{2,1,0:T(1,128)} %broadcast_in_dim.2), calls=%async_computation.4 | async-start | bytes 4096 | tf_op jit(solution)/shard_map/all_to_all | solution.py:34
  138.2 0.5 convert_bitcast_fusion.1
  138.7 0.1 copy.54
  138.8 0.1 copy.55
  138.9 10.6 %all-to-all-done.4 = f32[4,1,96]{2,1,0:T(1,128)S(1)} async-done(((f32[4,1,96]{2,1,0:T(1,128)}), f32[4,1,96]{2,1,0:T(1,128)S(1)}, u32[]{:S(2)}, u32[]{:S(2)}) %all-to-all-start.4) | async-done | bytes 1568 | tf_op jit(solution)/shard_map/all_to_all | solution.py:34
  149.6 0.7 convert_bitcast_fusion
  150.3 0.7 fusion
  151.0 0.7 concatenate.7
  151.8 63.6 %all-gather.2.cloned.1.call-done = bf16[768,1538]{1,0:T(8,128)(2,1)} async-done(((bf16[24,1538]{1,0:T(8,128)(2,1)}), bf16[768,1538]{1,0:T(8,128)(2,1)}) %all-gather.2.cloned.1.call-update) | async-done | bytes 2362384 | tf_op jit(solution)/shard_map/all_gather | solution.py:54
  215.4 2.8 %slice_bitcast_fusion = (bf16[768,768]{0,1:T(8,128)(2,1)S(1)}, bf16[768,768]{1,0:T(8,128)(2,1)}) fusion(bf16[768,1538]{1,0:T(8,128)(2,1)} %all-gather.2.cloned.1.call-done), kind=kLoop, calls=%fused_computation | loop fusion | bytes 4718592 | tf_op jit(solution)/shard_map/transpose | solution.py:57
  218.2 1.4 copy.56
  219.6 1.9 slice_reduce_fusion
  (23 shorter events, 0.4 us)
Async XLA Ops:
  8.6 11.5 %all-to-all-start.5 = ((f32[2,1,384]{2,1,0:T(1,128)}), f32[2,1,384]{2,1,0:T(1,128)S(1)}, u32[]{:S(2)}, u32[]{:S(2)}) async-start(f32[2,1,384]{2,1,0:T(1,128)} %reshape.64), calls=%async_computation.5 | async-start | bytes 6144 | tf_op jit(solution)/shard_map/all_to_all | solution.py:20
  20.2 13.3 %all-to-all-start.7 = ((f32[2,1,384]{2,1,0:T(1,128)}), f32[2,1,384]{2,1,0:T(1,128)S(1)}, u32[]{:S(2)}, u32[]{:S(2)}) async-start(f32[2,1,384]{2,1,0:T(1,128)} %reshape.66), calls=%async_computation.7 | async-start | bytes 6144 | tf_op jit(solution)/shard_map/all_to_all | solution.py:20
  33.4 6.3 %copy-start = (f32[2,16,768,24]{2,3,1,0:T(8,128)S(1)}, f32[2,16,768,24]{2,3,1,0:T(8,128)}, u32[]{:S(2)}) copy-start(f32[2,16,768,24]{2,3,1,0:T(8,128)} %copy.49) | copy-start | bytes 7077892
  45.4 10.2 %all-to-all-start.6 = ((f32[16,1,24]{2,1,0:T(1,128)}), f32[16,1,24]{2,1,0:T(1,128)S(1)}, u32[]{:S(2)}, u32[]{:S(2)}) async-start(f32[16,1,24]{2,1,0:T(1,128)} %bitcast.9), calls=%async_computation.6 | async-start | bytes 16384 | tf_op jit(solution)/shard_map/all_to_all | solution.py:28
  55.5 10.2 %all-to-all-start.8 = ((f32[16,1,24]{2,1,0:T(1,128)}), f32[16,1,24]{2,1,0:T(1,128)S(1)}, u32[]{:S(2)}, u32[]{:S(2)}) async-start(f32[16,1,24]{2,1,0:T(1,128)} %bitcast.12), calls=%async_computation.8 | async-start | bytes 16384 | tf_op jit(solution)/shard_map/all_to_all | solution.py:28
  65.7 28.0 %all-to-all-start.1 = ((f32[16,24,768]{2,1,0:T(8,128)}), f32[16,24,768]{2,1,0:T(8,128)S(1)}, u32[]{:S(2)}, u32[]{:S(2)}) async-start(f32[16,24,768]{2,1,0:T(8,128)} %reduce_sum.117), calls=%async_computation.1 | async-start | bytes 2359296 | tf_op jit(solution)/shard_map/all_to_all | solution.py:28
  70.6 31.4 %copy-start.2 = (f32[24,768]{1,0:T(8,128)S(1)}, f32[24,768]{1,0:T(8,128)}, u32[]{:S(2)}) copy-start(f32[24,768]{1,0:T(8,128)} %param.12) | copy-start | bytes 221188
  70.6 31.5 %copy-start.1 = (f32[768,24]{0,1:T(8,128)S(1)}, f32[768,24]{0,1:T(8,128)}, u32[]{:S(2)}) copy-start(f32[768,24]{0,1:T(8,128)} %param.13) | copy-start | bytes 221188
  70.7 31.7 %copy-start.3 = (f32[24]{0:T(128)S(1)}, f32[24]{0:T(128)}, u32[]{:S(2)}) copy-start(f32[24]{0:T(128)} %param.14) | copy-start | bytes 292
  70.7 67.6 %copy-start.4 = (f32[24]{0:T(128)S(1)}, f32[24]{0:T(128)}, u32[]{:S(2)}) copy-start(f32[24]{0:T(128)} %param.15) | copy-start | bytes 292
  93.7 32.8 %all-to-all-start.3 = ((f32[16,768,24]{1,2,0:T(8,128)}), f32[16,768,24]{1,2,0:T(8,128)S(1)}, u32[]{:S(2)}, u32[]{:S(2)}) async-start(f32[16,768,24]{1,2,0:T(8,128)} %reduce_sum.122), calls=%async_computation.3 | async-start | bytes 2359296 | tf_op jit(solution)/shard_map/all_to_all | solution.py:28
  127.3 22.2 %all-to-all-start.4 = ((f32[4,1,96]{2,1,0:T(1,128)}), f32[4,1,96]{2,1,0:T(1,128)S(1)}, u32[]{:S(2)}, u32[]{:S(2)}) async-start(f32[4,1,96]{2,1,0:T(1,128)} %broadcast_in_dim.2), calls=%async_computation.4 | async-start | bytes 4096 | tf_op jit(solution)/shard_map/all_to_all | solution.py:34
  138.2 77.2 %all-gather.2.cloned.1.call-start = ((), (), s32[]{:S(2)}) async-start(), calls=%async_computation.9 | async-start | bytes 2635776 | tf_op jit(solution)/shard_map/all_gather | solution.py:54
Sparse Core Ops, SparseCore 0:
  151.9 63.4 all-gather.1
where the time goes:
time: 229 us; the launch traced here: 228 us
  waiting for transfers between devices  130 us (57%)
  starting transfers between devices  43.3 us (19%)
  local copies, waits for them, and re-layouts  18 us (8%)
  between operations  14.2 us (6%)
  blocking collectives  11.9 us (5%)
  other arithmetic  11.5 us (5%)
    all_gather x1, waiting for transfers between devices, gather_turned(): whole, at, outs = (lax.all_gather(both, axis, axis=0, tiled=True), 0, [])  63.6 us
    all_to_all x4, waiting for transfers between devices, sum_by_axis(): lax.all_to_all(nearer, far, split_axis=0, concat_axis=0, tiled=True)  55.4 us
    all_to_all x4, starting transfers between devices, sum_by_axis(): lax.all_to_all(nearer, far, split_axis=0, concat_axis=0, tiled=True)  19 us
    all_to_all x2, starting transfers between devices, sum_at_owner(): tiles = lax.all_to_all(split_up(shard, dim, count), axis, 0, 0, tiled=True)  13.3 us
    all_to_all x2, blocking collectives, sum_at_owner(): tiles = lax.all_to_all(split_up(shard, dim, count), axis, 0, 0, tiled=True)  11.9 us
    all_to_all x1, starting transfers between devices, from_everyone(): lax.all_to_all(jnp.broadcast_to(shard[None], (count, *shard.shape)), axis...  10.9 us
    all_to_all x1, waiting for transfers between devices, from_everyone(): lax.all_to_all(jnp.broadcast_to(shard[None], (count, *shard.shape)), axis...  10.6 us
    unnamed x16, local copies, waits for them, and re-layouts  6 us
  transfers between devices with their start and end apart: 8, of which 6 were waited for; matrix products, arithmetic and copies ran while one was open for 8% of the time, Pallas kernels for 0%

commit v1 on v0

--- a/solution.py
+++ b/solution.py
@@ -51,7 +51,13 @@
 def gather_turned(arrays, axis, dims):
     turned = [jnp.moveaxis(a, dim, 0) for a, dim in zip(arrays, dims)]
     both = jnp.concatenate([t.reshape(len(t), -1) for t in turned], axis=1)
-    whole, at, outs = (lax.all_gather(both, axis, axis=0, tiled=True), 0, [])
+    whole, at, outs = (
+        jnp.concatenate(
+            lax.all_to_all(jnp.stack([both] * lax.axis_size(axis)), axis, 0, 0), axis=0
+        ),
+        0,
+        [],
+    )
     for t, dim in zip(turned, dims):
         section = whole[:, at : at + t[0].size].reshape(-1, *t.shape[1:])
         outs.append(jnp.moveaxis(section, 0, dim))

time: 229 us -> 221 us (0.965)
  blocking collectives: 11.9 us -> 83.5 us
  waiting for transfers between devices: 130 us -> 65.9 us
  between operations: 14.2 us -> 0.77 us
  local copies, waits for them, and re-layouts: 18 us -> 14.9 us
    all_to_all x0 -> x1, blocking collectives: none -> 71.6 us  [gather_turned(): lax.all_to_all(jnp.stack([both] * lax.axis_size(axis)), axis, 0, 0)]
    all_gather x1 -> x0, waiting for transfers between devices: 63.6 us -> none  [gather_turned(): whole, at, outs = (lax.all_gather(both, axis, axis=0, tiled=True), 0, [])]
  transfers between devices with their start and end apart: 8 -> 7, of which waited for: 6 -> 5; matrix products, arithmetic and copies ran while one was open for 8% -> 9% of each run, Pallas kernels for 0% -> 0%
where the time goes in v1:
time: 221 us; the launch traced here: 220 us
  blocking collectives  83.5 us (38%)
  waiting for transfers between devices  65.9 us (30%)
  starting transfers between devices  43.3 us (20%)
  local copies, waits for them, and re-layouts  14.9 us (7%)
  other arithmetic  11.5 us (5%)
    all_to_all x1, blocking collectives, gather_turned(): lax.all_to_all(jnp.stack([both] * lax.axis_size(axis)), axis, 0, 0)  71.6 us
    all_to_all x4, waiting for transfers between devices, sum_by_axis(): lax.all_to_all(nearer, far, split_axis=0, concat_axis=0, tiled=True)  55.4 us
    all_to_all x4, starting transfers between devices, sum_by_axis(): lax.all_to_all(nearer, far, split_axis=0, concat_axis=0, tiled=True)  19 us
    all_to_all x2, starting transfers between devices, sum_at_owner(): tiles = lax.all_to_all(split_up(shard, dim, count), axis, 0, 0, tiled=True)  13.3 us
    all_to_all x2, blocking collectives, sum_at_owner(): tiles = lax.all_to_all(split_up(shard, dim, count), axis, 0, 0, tiled=True)  11.9 us
    all_to_all x1, starting transfers between devices, from_everyone(): lax.all_to_all(jnp.broadcast_to(shard[None], (count, *shard.shape)), axis...  10.9 us
    all_to_all x1, waiting for transfers between devices, from_everyone(): lax.all_to_all(jnp.broadcast_to(shard[None], (count, *shard.shape)), axis...  10.6 us
    unnamed x16, local copies, waits for them, and re-layouts  6 us
  transfers between devices with their start and end apart: 7, of which 5 were waited for; matrix products, arithmetic and copies ran while one was open for 9% of the time, Pallas kernels for 0%

profile of v1, /device:TPU:1, one launch (start us, length us, event | category | flops | bytes accessed | tf_op | source)
XLA Modules:
  0.0 219.8 jit_solution(13088483646720810155)
XLA Ops:
  0.6 0.7 reduce.3
  1.3 0.1 reshape_reshape_squeeze.10
  1.4 0.7 reshape.70
  2.1 10.0 %all-to-all-start.5 = ((f32[2,1,384]{2,1,0:T(1,128)}), f32[2,1,384]{2,1,0:T(1,128)S(1)}, u32[]{:S(2)}, u32[]{:S(2)}) async-start(f32[2,1,384]{2,1,0:T(1,128)} %reshape.70), calls=%async_computation.5 | async-start | bytes 6144 | tf_op jit(solution)/shard_map/all_to_all | solution.py:20
  12.2 0.7 reduce.4
  12.9 0.1 reshape_reshape_squeeze.11
  13.0 0.7 reshape.72
  13.6 3.2 %all-to-all-start.7 = ((f32[2,1,384]{2,1,0:T(1,128)}), f32[2,1,384]{2,1,0:T(1,128)S(1)}, u32[]{:S(2)}, u32[]{:S(2)}) async-start(f32[2,1,384]{2,1,0:T(1,128)} %reshape.72), calls=%async_computation.7 | async-start | bytes 6144 | tf_op jit(solution)/shard_map/all_to_all | solution.py:20
  16.9 0.5 broadcast.26
  17.4 0.7 reduce.9
  18.0 0.1 reshape.71
  18.1 1.8 copy.52
  20.0 3.0 %copy.53 = f32[1,768,768]{1,2,0:T(8,128)} copy(f32[1,768,768]{2,1,0:T(8,128)} %param.9) | data formatting | bytes 4718592 | tf_op args[1]
  23.0 3.3 %copy.54 = f32[2,16,768,24]{2,3,1,0:T(8,128)} copy(f32[2,16,768,24]{2,3,0,1:T(8,128)} %bitcast.26) | data formatting | bytes 4718592 | tf_op jit(solution)/shard_map/transpose | solution.py:15
  26.3 0.6 reduce_sum.126
  26.9 6.3 %all_to_all.59 = f32[2,16,24,768]{3,2,1,0:T(8,128)} all-to-all(f32[2,16,24,768]{3,2,1,0:T(8,128)S(1)} %copy.52), channel_id=1, replica_groups=mesh['ens'=4,'replica_0'=4,'replica_1'=4,'replica_2'=2,'model'=4] {'repl..., dimensions={0} | all-to-all | bytes 4718592 | tf_op jit(solution)/shard_map/all_to_all | solution.py:20
  33.2 5.6 %all_to_all.60 = f32[2,16,768,24]{2,3,1,0:T(8,128)S(1)} all-to-all(f32[2,16,768,24]{2,3,1,0:T(8,128)S(1)} %copy-done), channel_id=1, replica_groups=mesh['ens'=4,'replica_0'=4,'replica_1'=4,'replica_2'=2,'model'=4] {'repl..., dimensions={0} | all-to-all | bytes 4718592 | tf_op jit(solution)/shard_map/all_to_all | solution.py:20
  38.8 3.5 %all-to-all-start.6 = ((f32[16,1,24]{2,1,0:T(1,128)}), f32[16,1,24]{2,1,0:T(1,128)S(1)}, u32[]{:S(2)}, u32[]{:S(2)}) async-start(f32[16,1,24]{2,1,0:T(1,128)} %bitcast.9), calls=%async_computation.6 | async-start | bytes 16384 | tf_op jit(solution)/shard_map/all_to_all | solution.py:28
  42.3 0.7 reduce.10
  43.1 0.6 reduce_sum.128
  43.7 5.3 %all-to-all-done.6 = f32[16,1,24]{2,1,0:T(1,128)S(1)} async-done(((f32[16,1,24]{2,1,0:T(1,128)}), f32[16,1,24]{2,1,0:T(1,128)S(1)}, u32[]{:S(2)}, u32[]{:S(2)}) %all-to-all-start.6) | async-done | bytes 1568 | tf_op jit(solution)/shard_map/all_to_all | solution.py:28
  49.0 3.5 %all-to-all-start.8 = ((f32[16,1,24]{2,1,0:T(1,128)}), f32[16,1,24]{2,1,0:T(1,128)S(1)}, u32[]{:S(2)}, u32[]{:S(2)}) async-start(f32[16,1,24]{2,1,0:T(1,128)} %bitcast.12), calls=%async_computation.8 | async-start | bytes 16384 | tf_op jit(solution)/shard_map/all_to_all | solution.py:28
  52.5 3.0 %reduce_sum.117 = f32[16,24,768]{2,1,0:T(8,128)} reduce(f32[2,16,24,768]{3,2,1,0:T(8,128)} %all_to_all.59, f32[]{:T(128)} %constant.5.clone.1), dimensions={0}, to_apply=%region_0.0 | reduce | flops 294912 | bytes 3538948 | tf_op jit(solution)/shard_map/reduce_sum | solution.py:21
  55.4 3.7 %all-to-all-done.8 = f32[16,1,24]{2,1,0:T(1,128)S(1)} async-done(((f32[16,1,24]{2,1,0:T(1,128)}), f32[16,1,24]{2,1,0:T(1,128)S(1)}, u32[]{:S(2)}, u32[]{:S(2)}) %all-to-all-start.8) | async-done | bytes 1568 | tf_op jit(solution)/shard_map/all_to_all | solution.py:28
  59.1 3.7 %all-to-all-start.1 = ((f32[16,24,768]{2,1,0:T(8,128)}), f32[16,24,768]{2,1,0:T(8,128)S(1)}, u32[]{:S(2)}, u32[]{:S(2)}) async-start(f32[16,24,768]{2,1,0:T(8,128)} %reduce_sum.117), calls=%async_computation.1 | async-start | bytes 2359296 | tf_op jit(solution)/shard_map/all_to_all | solution.py:28
  62.8 1.3 reduce_sum.122
  64.1 23.0 %all-to-all-done.1 = f32[16,24,768]{2,1,0:T(8,128)S(1)} async-done(((f32[16,24,768]{2,1,0:T(8,128)}), f32[16,24,768]{2,1,0:T(8,128)S(1)}, u32[]{:S(2)}, u32[]{:S(2)}) %all-to-all-start.1) | async-done | bytes 1179680 | tf_op jit(solution)/shard_map/all_to_all | solution.py:28
  87.1 8.4 %all-to-all-start.3 = ((f32[16,768,24]{1,2,0:T(8,128)}), f32[16,768,24]{1,2,0:T(8,128)S(1)}, u32[]{:S(2)}, u32[]{:S(2)}) async-start(f32[16,768,24]{1,2,0:T(8,128)} %reduce_sum.122), calls=%async_computation.3 | async-start | bytes 2359296 | tf_op jit(solution)/shard_map/all_to_all | solution.py:28
  95.5 0.1 multiply_reduce_fusion.3
  95.7 0.1 multiply_reduce_fusion.2
  95.8 0.5 convert_bitcast_fusion.2
  96.4 0.1 multiply_reduce_fusion.1
  96.6 23.3 %all-to-all-done.3 = f32[16,768,24]{1,2,0:T(8,128)S(1)} async-done(((f32[16,768,24]{1,2,0:T(8,128)}), f32[16,768,24]{1,2,0:T(8,128)S(1)}, u32[]{:S(2)}, u32[]{:S(2)}) %all-to-all-start.3) | async-done | bytes 1179680 | tf_op jit(solution)/shard_map/all_to_all | solution.py:28
  120.0 0.1 multiply_reduce_fusion
  120.2 0.6 broadcast_in_dim.2
  120.7 10.9 %all-to-all-start.4 = ((f32[4,1,96]{2,1,0:T(1,128)}), f32[4,1,96]{2,1,0:T(1,128)S(1)}, u32[]{:S(2)}, u32[]{:S(2)}) async-start(f32[4,1,96]{2,1,0:T(1,128)} %broadcast_in_dim.2), calls=%async_computation.4 | async-start | bytes 4096 | tf_op jit(solution)/shard_map/all_to_all | solution.py:34
  131.7 0.5 convert_bitcast_fusion.1
  132.2 0.1 copy.59
  132.3 0.1 copy.60
  132.4 10.6 %all-to-all-done.4 = f32[4,1,96]{2,1,0:T(1,128)S(1)} async-done(((f32[4,1,96]{2,1,0:T(1,128)}), f32[4,1,96]{2,1,0:T(1,128)S(1)}, u32[]{:S(2)}, u32[]{:S(2)}) %all-to-all-start.4) | async-done | bytes 1568 | tf_op jit(solution)/shard_map/all_to_all | solution.py:34
  143.1 0.7 convert_bitcast_fusion
  143.8 0.7 fusion
  144.5 0.1 concatenate.7
  144.6 0.2 stack.2
  144.8 71.6 %all_to_all.61 = bf16[32,24,1538]{2,1,0:T(8,128)(2,1)S(1)} all-to-all(bf16[32,24,1538]{2,1,0:T(8,128)(2,1)S(1)} %stack.2), channel_id=1, replica_groups=mesh['ens'=4,'replica_0'=4,'replica_1'=4,'replica_2'=2,'model'=4] {'repl..., dimensions={0} | all-to-all | bytes 4724736 | tf_op jit(solution)/shard_map/all_to_all | solution.py:56
  216.3 0.9 slice_reduce_fusion
  217.2 1.2 slice_bitcast_fusion
  218.4 1.4 copy.61
  (22 shorter events, 0.5 us)
Async XLA Ops:
  2.1 11.5 %all-to-all-start.5 = ((f32[2,1,384]{2,1,0:T(1,128)}), f32[2,1,384]{2,1,0:T(1,128)S(1)}, u32[]{:S(2)}, u32[]{:S(2)}) async-start(f32[2,1,384]{2,1,0:T(1,128)} %reshape.70), calls=%async_computation.5 | async-start | bytes 6144 | tf_op jit(solution)/shard_map/all_to_all | solution.py:20
  13.6 13.3 %all-to-all-start.7 = ((f32[2,1,384]{2,1,0:T(1,128)}), f32[2,1,384]{2,1,0:T(1,128)S(1)}, u32[]{:S(2)}, u32[]{:S(2)}) async-start(f32[2,1,384]{2,1,0:T(1,128)} %reshape.72), calls=%async_computation.7 | async-start | bytes 6144 | tf_op jit(solution)/shard_map/all_to_all | solution.py:20
  26.9 6.3 %copy-start = (f32[2,16,768,24]{2,3,1,0:T(8,128)S(1)}, f32[2,16,768,24]{2,3,1,0:T(8,128)}, u32[]{:S(2)}) copy-start(f32[2,16,768,24]{2,3,1,0:T(8,128)} %copy.54) | copy-start | bytes 7077892
  38.8 10.2 %all-to-all-start.6 = ((f32[16,1,24]{2,1,0:T(1,128)}), f32[16,1,24]{2,1,0:T(1,128)S(1)}, u32[]{:S(2)}, u32[]{:S(2)}) async-start(f32[16,1,24]{2,1,0:T(1,128)} %bitcast.9), calls=%async_computation.6 | async-start | bytes 16384 | tf_op jit(solution)/shard_map/all_to_all | solution.py:28
  49.0 10.2 %all-to-all-start.8 = ((f32[16,1,24]{2,1,0:T(1,128)}), f32[16,1,24]{2,1,0:T(1,128)S(1)}, u32[]{:S(2)}, u32[]{:S(2)}) async-start(f32[16,1,24]{2,1,0:T(1,128)} %bitcast.12), calls=%async_computation.8 | async-start | bytes 16384 | tf_op jit(solution)/shard_map/all_to_all | solution.py:28
  59.1 28.0 %all-to-all-start.1 = ((f32[16,24,768]{2,1,0:T(8,128)}), f32[16,24,768]{2,1,0:T(8,128)S(1)}, u32[]{:S(2)}, u32[]{:S(2)}) async-start(f32[16,24,768]{2,1,0:T(8,128)} %reduce_sum.117), calls=%async_computation.1 | async-start | bytes 2359296 | tf_op jit(solution)/shard_map/all_to_all | solution.py:28
  64.1 31.4 %copy-start.2 = (f32[24,768]{1,0:T(8,128)S(1)}, f32[24,768]{1,0:T(8,128)}, u32[]{:S(2)}) copy-start(f32[24,768]{1,0:T(8,128)} %param.12) | copy-start | bytes 221188
  64.1 31.5 %copy-start.1 = (f32[768,24]{0,1:T(8,128)S(1)}, f32[768,24]{0,1:T(8,128)}, u32[]{:S(2)}) copy-start(f32[768,24]{0,1:T(8,128)} %param.13) | copy-start | bytes 221188
  64.1 31.7 %copy-start.3 = (f32[24]{0:T(128)S(1)}, f32[24]{0:T(128)}, u32[]{:S(2)}) copy-start(f32[24]{0:T(128)} %param.14) | copy-start | bytes 292
  64.1 67.6 %copy-start.4 = (f32[24]{0:T(128)S(1)}, f32[24]{0:T(128)}, u32[]{:S(2)}) copy-start(f32[24]{0:T(128)} %param.15) | copy-start | bytes 292
  87.1 32.8 %all-to-all-start.3 = ((f32[16,768,24]{1,2,0:T(8,128)}), f32[16,768,24]{1,2,0:T(8,128)S(1)}, u32[]{:S(2)}, u32[]{:S(2)}) async-start(f32[16,768,24]{1,2,0:T(8,128)} %reduce_sum.122), calls=%async_computation.3 | async-start | bytes 2359296 | tf_op jit(solution)/shard_map/all_to_all | solution.py:28
  120.7 22.2 %all-to-all-start.4 = ((f32[4,1,96]{2,1,0:T(1,128)}), f32[4,1,96]{2,1,0:T(1,128)S(1)}, u32[]{:S(2)}, u32[]{:S(2)}) async-start(f32[4,1,96]{2,1,0:T(1,128)} %broadcast_in_dim.2), calls=%async_computation.4 | async-start | bytes 4096 | tf_op jit(solution)/shard_map/all_to_all | solution.py:34
